TPU v7x, 32 devices: a whole 2x2x4 slice. The times are simulated.
32 devices in a mesh: dp: 2 (over core), tensor: 16 (over z, y, x).
Axes of the slice: x: 2, y: 2, z: 4, core: 2. Of those that a mesh axis runs over, the one named last changes fastest.
Arguments:
- inputs: bfloat16 [768, 6144], P(('dp', 'tensor')), may hold values from -0.29882812 to 0.29882812
- norm_gain: float32 [6144], replicated, may hold values from 0.1 to 1.9
- norm_bias: float32 [6144], replicated, may hold values from -3 to 3
- query_grad: bfloat16 [768, 12288], P('dp', 'tensor'), may hold values from -0.119628906 to 0.119628906
- stream_grad: bfloat16 [768, 6144], P(('dp', 'tensor')), may hold values from -2.390625 to 2.390625
- query_weight: bfloat16 [6144, 12288], P(None, 'tensor'), may hold values from -0.0546875 to 0.0546875
Outputs:
- input_grad: bfloat16 [768, 6144], P(('dp', 'tensor'))
- weight_grad: bfloat16 [6144, 12288], P(None, 'tensor')
All inputs are finite; a program needn't handle non-finite values.
Results may differ from a plain program's by a relative error of at most 0.019.
Values may be sent and summed in bfloat16 or wider, within the bound.
No kernel may reach another device: no remote copies, remote signals or barrier semaphores. Data moves between devices by JAX's collectives and lax.ppermute only.
A program may use at most 128 MiB of HBM per device.

v0:
```python
import jax
import jax.numpy as jnp
from jax import lax
from jax.sharding import PartitionSpec as P

epsilon = 1e-05


def normalize(values, norm_gain, norm_bias):
    as_float = values.astype(jnp.float32)
    centre = jnp.mean(as_float, axis=-1, keepdims=True)
    offsets = as_float - centre
    variance = jnp.mean(offsets * offsets, axis=-1, keepdims=True)
    inverse = lax.rsqrt(variance + epsilon)
    scaled = offsets * inverse
    normed = (scaled * norm_gain + norm_bias).astype(jnp.bfloat16)
    return (scaled, inverse, normed)


def norm_backward(scaled, inverse, normed_grad, norm_gain, stream_grad):
    weighted = normed_grad * norm_gain
    first_moment = jnp.mean(weighted, axis=-1, keepdims=True)
    second_moment = jnp.mean(weighted * scaled, axis=-1, keepdims=True)
    result = stream_grad.astype(jnp.float32) + inverse * (
        weighted - first_moment - scaled * second_moment
    )
    return result.astype(jnp.bfloat16)


def shards(inputs, norm_gain, norm_bias, query_grad, stream_grad, query_weight):
    scaled, inverse, normed = normalize(inputs, norm_gain, norm_bias)
    unused_scaled, unused_inverse, piece_normed = normalize(
        lax.all_gather(inputs, "tensor", axis=0, tiled=True), norm_gain, norm_bias
    )
    grad_rows = query_grad
    weight_grad = lax.psum(
        lax.dot_general(
            piece_normed, grad_rows, (((0,), (0,)), ((), ())), preferred_element_type=jnp.float32
        ).astype(jnp.bfloat16),
        "dp",
    )
    grad_rows = query_grad
    normed_grad = lax.psum_scatter(
        lax.dot_general(
            grad_rows, query_weight, (((1,), (1,)), ((), ())), preferred_element_type=jnp.float32
        ).astype(jnp.bfloat16),
        "tensor",
        scatter_dimension=0,
        tiled=True,
    ).astype(jnp.float32)
    input_grad = norm_backward(scaled, inverse, normed_grad, norm_gain, stream_grad)
    return (input_grad, weight_grad)


def solution(mesh):
    placed = (
        P(("dp", "tensor"), None),
        P(),
        P(),
        P("dp", "tensor"),
        P(("dp", "tensor"), None),
        P(None, "tensor"),
    )
    return jax.shard_map(
        shards,
        mesh=mesh,
        in_specs=placed,
        out_specs=(P(("dp", "tensor"), None), P(None, "tensor")),
        check_vma=False,
    )
```

profile of v0, /device:TPU:0, one launch (start us, length us, event | category | flops | bytes accessed | tf_op | source)
XLA Modules:
  0.0 294.0 jit_solution(8488594455797029391)
XLA Ops:
  7.2 0.0 copy-start
  7.2 0.0 all-gather.2.cloned.1.call-start
  7.2 0.7 all-gather.2.cloned.1.call-update
  7.9 0.0 reduce-scatter.2.cloned.1.call-start
  8.0 0.3 copy-done
  8.2 11.6 %convolution_convert_fusion.1 = bf16[384,6144]{1,0:T(8,128)(2,1)} fusion(bf16[384,768]{1,0:T(8,128)(2,1)S(1)} %copy-done, bf16[6144,768]{1,0:T(8,128)(2,1)} %param.11), kind=kOutput, calls=%fused_computation.9 | convolution fusion | flops 3626237952 | bytes 14745600 | tf_op jit(solution)/shard_map/dot_general | solution.py:44
  19.8 0.0 reduce-scatter.2.cloned.1.call-update
  19.8 0.0 all-reduce.2.cloned.1.call-start
  19.9 73.3 %all-gather.2.cloned.1.call-done = bf16[384,6144]{1,0:T(8,128)(2,1)} async-done(((bf16[24,6144]{1,0:T(8,128)(2,1)}), bf16[384,6144]{1,0:T(8,128)(2,1)}) %all-gather.2.cloned.1.call-update) | async-done | bytes 4718608 | tf_op jit(solution)/shard_map/all_gather | solution.py:33
  93.2 3.2 %convert_reduce_fusion = f32[384]{0:T(512)S(1)} fusion(bf16[384,6144]{1,0:T(8,128)(2,1)} %all-gather.2.cloned.1.call-done), kind=kLoop, calls=%fused_computation.1 | loop fusion | flops 4718208 | bytes 4720128 | tf_op jit(solution)/shard_map/reduce_sum | solution.py:11
  96.4 3.7 %fusion.2 = f32[384]{0:T(512)S(1)} fusion(bf16[384,6144]{1,0:T(8,128)(2,1)} %all-gather.2.cloned.1.call-done, f32[384]{0:T(512)S(1)} %broadcast_multiply_fusion), kind=kLoop, calls=%fused_computation.5 | loop fusion | flops 9436800 | bytes 4721664 | tf_op jit(solution)/shard_map/reduce_sum | solution.py:13
  100.2 0.0 copy-done.4
  100.2 0.0 copy-done.5
  100.2 8.1 %convolution_convert_fusion = bf16[6144,768]{1,0:T(8,128)(2,1)} fusion(bf16[384,768]{1,0:T(8,128)(2,1)S(1)} %copy-done, bf16[384,6144]{1,0:T(8,128)(2,1)S(1)} %copy-done.1, f32[6144]{0:T(1024)S(1)} %copy-done.5, f32[6144]{0:T(1024)S(1)} %copy-done.4, f32[384]{0:T(512)S(1)} %add_rsqrt_fusion, f32[384]{0:T(512)S(1)} %broadcast_multiply_fusion), kind=kOutput, calls=%fused_computation.4 | convolution fusion | flops 3642753024 | bytes 14797824 | tf_op jit(solution)/shard_map/dot_general | solution.py:37
  108.3 0.0 all-reduce.2.cloned.1.call-update
  108.3 0.9 copy-done.2
  109.2 0.2 convert_reduce_fusion.1
  109.4 0.3 fusion.20
  109.7 126.6 %reduce-scatter.2.cloned.1.call-done = bf16[24,6144]{1,0:T(8,128)(2,1)} async-done(((bf16[384,6144]{1,0:T(8,128)(2,1)}), bf16[24,6144]{1,0:T(8,128)(2,1)}) %reduce-scatter.2.cloned.1.call-update) | async-done | bytes 294928 | tf_op jit(solution)/shard_map/reduce_scatter | solution.py:43
  236.2 1.2 fusion.21
  237.5 0.0 copy-done.3
  237.5 2.0 fusion.19
  239.5 39.9 %all-reduce.2.cloned.1.call-done = bf16[6144,768]{1,0:T(8,128)(2,1)} async-done(((bf16[6144,768]{1,0:T(8,128)(2,1)}), bf16[6144,768]{1,0:T(8,128)(2,1)}) %all-reduce.2.cloned.1.call-update) | async-done | bytes 9437200 | tf_op jit(solution)/shard_map/psum | solution.py:36
  279.4 8.0 %copy.9 = bf16[6144,768]{1,0:T(8,128)(2,1)} copy(bf16[6144,768]{1,0:T(8,128)(2,1)} %all-reduce.2.cloned.1.call-done) | data formatting | bytes 18874368
  (11 shorter events, 0.0 us)
Async XLA Ops:
  7.2 1.1 copy-start
  7.2 86.1 %all-gather.2.cloned.1.call-start = ((), (), s32[]{:S(2)}) async-start(), calls=%async_computation.2 | async-start | bytes 5013504 | tf_op jit(solution)/shard_map/all_gather | solution.py:33
  7.9 228.3 %reduce-scatter.2.cloned.1.call-start = ((), (), s32[]{:S(2)}) async-start(), calls=%async_computation.1 | async-start | bytes 5013504 | tf_op jit(solution)/shard_map/reduce_scatter | solution.py:43
  19.8 80.3 %copy-start.4 = (f32[6144]{0:T(1024)S(1)}, f32[6144]{0:T(1024)}, u32[]{:S(2)}) copy-start(f32[6144]{0:T(1024)} %param.7) | copy-start | bytes 73732
  19.8 80.4 %copy-start.5 = (f32[6144]{0:T(1024)S(1)}, f32[6144]{0:T(1024)}, u32[]{:S(2)}) copy-start(f32[6144]{0:T(1024)} %param.8) | copy-start | bytes 73732
  19.8 259.6 %all-reduce.2.cloned.1.call-start = ((), (), s32[]{:S(2)}) async-start(), calls=%async_computation.3 | async-start | bytes 18874368 | tf_op jit(solution)/shard_map/psum | solution.py:36
  93.2 6.9 %copy-start.1 = (bf16[384,6144]{1,0:T(8,128)(2,1)S(1)}, bf16[384,6144]{1,0:T(8,128)(2,1)}, u32[]{:S(2)}) copy-start(bf16[384,6144]{1,0:T(8,128)(2,1)} %all-gather.2.cloned.1.call-done) | copy-start | bytes 14155780
  108.3 1.0 copy-start.2
  108.3 129.2 %copy-start.3 = (bf16[24,6144]{1,0:T(8,128)(2,1)S(1)}, bf16[24,6144]{1,0:T(8,128)(2,1)}, u32[]{:S(2)}) copy-start(bf16[24,6144]{1,0:T(8,128)(2,1)} %param.10) | copy-start | bytes 884740
Sparse Core Ops, SparseCore 0:
  10.8 82.3 all-gather.1
  98.4 137.8 reduce-scatter.1
  239.3 40.0 all-reduce.1
where the time goes:
time: 294 us
  waiting for transfers between devices  241 us (82%)
  matrix products  19.7 us (7%)
  between operations  13.8 us (5%)
  other arithmetic  10.6 us (4%)
  local copies, waits for them, and re-layouts  9.26 us (3%)
    reduce_scatter x1, waiting for transfers between devices, shards(): lax.psum_scatter(lax.dot_general(grad_rows, query_weight, (((1,), (1,)),...  127 us
    all_gather x1, waiting for transfers between devices, shards(): lax.all_gather(inputs, 'tensor', axis=0, tiled=True)  73.3 us
    psum x1, waiting for transfers between devices, shards(): lax.psum(lax.dot_general(piece_normed, grad_rows, (((0,), (0,)), ((), ())...  39.9 us
    dot_general x1, matrix products, shards(): lax.dot_general(grad_rows, query_weight, (((1,), (1,)), ((), ())), prefer...  11.6 us
    unnamed x13, local copies, waits for them, and re-layouts  9.26 us
    dot_general x1, matrix products, shards(): lax.dot_general(piece_normed, grad_rows, (((0,), (0,)), ((), ())), prefer...  8.08 us
  transfers between devices with their start and end apart: 3, of which 3 were waited for; matrix products, arithmetic and copies ran while one was open for 10% of the time, Pallas kernels for 0%

commit v1 on v0

--- a/solution.py
+++ b/solution.py
@@ -33,11 +33,17 @@
         lax.all_gather(inputs, "tensor", axis=0, tiled=True), norm_gain, norm_bias
     )
     grad_rows = query_grad
-    weight_grad = lax.psum(
-        lax.dot_general(
-            piece_normed, grad_rows, (((0,), (0,)), ((), ())), preferred_element_type=jnp.float32
-        ).astype(jnp.bfloat16),
-        "dp",
+    weight_grad = jnp.sum(
+        lax.all_gather(
+            lax.dot_general(
+                piece_normed,
+                grad_rows,
+                (((0,), (0,)), ((), ())),
+                preferred_element_type=jnp.float32,
+            ).astype(jnp.bfloat16),
+            "dp",
+        ),
+        axis=0,
     )
     grad_rows = query_grad
     normed_grad = lax.psum_scatter(

time: 294 us -> 295 us (level)
  other arithmetic: 10.6 us -> 27.4 us
  waiting for transfers between devices: 241 us -> 232 us
  local copies, waits for them, and re-layouts: 9.26 us -> 1.23 us
    psum x1 -> x0, waiting for transfers between devices: 39.9 us -> none  [shards(): lax.psum(lax.dot_general(piece_normed, grad_rows, (((0,), (0,)), ((), ())...]
    all_gather x0 -> x1, waiting for transfers between devices: none -> 31.5 us  [shards(): lax.all_gather(lax.dot_general(piece_normed, grad_rows, (((0,), (0,)), ((...]
    reduce_sum x0 -> x1, other arithmetic: none -> 16.8 us  [shards(): jnp.sum(lax.all_gather(lax.dot_general(piece_normed, grad_rows, (((0,), (...]
    unnamed x13 -> x12, local copies, waits for them, and re-layouts: 9.26 us -> 1.23 us
where the time goes in v1:
time: 295 us; the launch traced here: 294 us
  waiting for transfers between devices  232 us (79%)
  other arithmetic  27.4 us (9%)
  matrix products  19.6 us (7%)
  between operations  13.8 us (5%)
    reduce_scatter x1, waiting for transfers between devices, shards(): lax.psum_scatter(lax.dot_general(grad_rows, query_weight, (((1,), (1,)),...  127 us
    all_gather x1, waiting for transfers between devices, shards(): lax.all_gather(inputs, 'tensor', axis=0, tiled=True)  73.4 us
    all_gather x1, waiting for transfers between devices, shards(): lax.all_gather(lax.dot_general(piece_normed, grad_rows, (((0,), (0,)), ((...  31.5 us
    reduce_sum x1, other arithmetic, shards(): jnp.sum(lax.all_gather(lax.dot_general(piece_normed, grad_rows, (((0,), (...  16.8 us
    dot_general x1, matrix products, shards(): lax.dot_general(grad_rows, query_weight, (((1,), (1,)), ((), ())), prefer...  11.5 us
    dot_general x1, matrix products, shards(): lax.dot_general(piece_normed, grad_rows, (((0,), (0,)), ((), ())), prefer...  8.08 us
  transfers between devices with their start and end apart: 3, of which 3 were waited for; matrix products, arithmetic and copies ran while one was open for 10% of the time, Pallas kernels for 0%

profile of v1, /device:TPU:0, one launch (start us, length us, event | category | flops | bytes accessed | tf_op | source)
XLA Modules:
  0.0 294.4 jit_solution(16958586223890224192)
XLA Ops:
  7.2 0.0 copy-start
  7.2 0.0 all-gather.4.cloned.1.call-start
  7.2 0.7 all-gather.4.cloned.1.call-update
  7.9 0.0 reduce-scatter.2.cloned.1.call-start
  8.0 0.3 copy-done
  8.2 11.5 %convolution_convert_fusion.1 = bf16[384,6144]{1,0:T(8,128)(2,1)} fusion(bf16[384,768]{1,0:T(8,128)(2,1)S(1)} %copy-done, bf16[6144,768]{1,0:T(8,128)(2,1)} %param.11), kind=kOutput, calls=%fused_computation.9 | convolution fusion | flops 3626237952 | bytes 14745600 | tf_op jit(solution)/shard_map/dot_general | solution.py:50
  19.8 0.0 reduce-scatter.2.cloned.1.call-update
  19.8 0.0 all-gather.6.cloned.1.call-start
  19.8 73.4 %all-gather.4.cloned.1.call-done = bf16[384,6144]{1,0:T(8,128)(2,1)} async-done(((bf16[24,6144]{1,0:T(8,128)(2,1)}), bf16[384,6144]{1,0:T(8,128)(2,1)}) %all-gather.4.cloned.1.call-update) | async-done | bytes 4718608 | tf_op jit(solution)/shard_map/all_gather | solution.py:33
  93.2 3.2 %convert_reduce_fusion = f32[384]{0:T(512)S(1)} fusion(bf16[384,6144]{1,0:T(8,128)(2,1)} %all-gather.4.cloned.1.call-done), kind=kLoop, calls=%fused_computation.1 | loop fusion | flops 4718208 | bytes 4720128 | tf_op jit(solution)/shard_map/reduce_sum | solution.py:11
  96.4 3.7 %fusion.2 = f32[384]{0:T(512)S(1)} fusion(bf16[384,6144]{1,0:T(8,128)(2,1)} %all-gather.4.cloned.1.call-done, f32[384]{0:T(512)S(1)} %broadcast_multiply_fusion), kind=kLoop, calls=%fused_computation.5 | loop fusion | flops 9436800 | bytes 4721664 | tf_op jit(solution)/shard_map/reduce_sum | solution.py:13
  100.2 0.0 copy-done.4
  100.2 0.0 copy-done.5
  100.2 0.0 copy-done.1
  100.2 8.1 %convolution_convert_fusion = bf16[6144,768]{1,0:T(8,128)(2,1)} fusion(bf16[384,768]{1,0:T(8,128)(2,1)S(1)} %copy-done, bf16[384,6144]{1,0:T(8,128)(2,1)S(1)} %copy-done.1, f32[6144]{0:T(1024)S(1)} %copy-done.5, f32[6144]{0:T(1024)S(1)} %copy-done.4, f32[384]{0:T(512)S(1)} %add_rsqrt_fusion, f32[384]{0:T(512)S(1)} %broadcast_multiply_fusion), kind=kOutput, calls=%fused_computation.4 | convolution fusion | flops 3642753024 | bytes 14797824 | tf_op jit(solution)/shard_map/dot_general | solution.py:38
  108.3 0.0 all-gather.6.cloned.1.call-update
  108.3 0.9 copy-done.2
  109.2 0.2 convert_reduce_fusion.1
  109.4 0.3 fusion.20
  109.7 126.6 %reduce-scatter.2.cloned.1.call-done = bf16[24,6144]{1,0:T(8,128)(2,1)} async-done(((bf16[384,6144]{1,0:T(8,128)(2,1)}), bf16[24,6144]{1,0:T(8,128)(2,1)}) %reduce-scatter.2.cloned.1.call-update) | async-done | bytes 294928 | tf_op jit(solution)/shard_map/reduce_scatter | solution.py:49
  236.3 1.2 fusion.21
  237.6 2.0 fusion.19
  239.5 31.5 %all-gather.6.cloned.1.call-done = bf16[12288,768]{1,0:T(8,128)(2,1)} async-done(((bf16[6144,768]{1,0:T(8,128)(2,1)}), bf16[12288,768]{1,0:T(8,128)(2,1)}) %all-gather.6.cloned.1.call-update) | async-done | bytes 18874384 | tf_op jit(solution)/shard_map/all_gather | solution.py:37
  271.0 16.8 %reduce_sum.72 = bf16[6144,768]{1,0:T(8,128)(2,1)} reduce(bf16[2,6144,768]{2,1,0:T(8,128)(2,1)} %bitcast.4, bf16[]{:T(256)} %constant.15.clone.1), dimensions={0}, to_apply=%region_7.0 | reduce | flops 4718592 | bytes 28311554 | tf_op jit(solution)/shard_map/reduce_sum | solution.py:36
  (11 shorter events, 0.0 us)
Async XLA Ops:
  7.2 1.1 copy-start
  7.2 86.1 %all-gather.4.cloned.1.call-start = ((), (), s32[]{:S(2)}) async-start(), calls=%async_computation.2 | async-start | bytes 5013504 | tf_op jit(solution)/shard_map/all_gather | solution.py:33
  7.9 228.4 %reduce-scatter.2.cloned.1.call-start = ((), (), s32[]{:S(2)}) async-start(), calls=%async_computation.1 | async-start | bytes 5013504 | tf_op jit(solution)/shard_map/reduce_scatter | solution.py:49
  19.8 80.4 %copy-start.4 = (f32[6144]{0:T(1024)S(1)}, f32[6144]{0:T(1024)}, u32[]{:S(2)}) copy-start(f32[6144]{0:T(1024)} %param.7) | copy-start | bytes 73732
  19.8 80.4 %copy-start.5 = (f32[6144]{0:T(1024)S(1)}, f32[6144]{0:T(1024)}, u32[]{:S(2)}) copy-start(f32[6144]{0:T(1024)} %param.8) | copy-start | bytes 73732
  19.8 251.3 %all-gather.6.cloned.1.call-start = ((), (), s32[]{:S(2)}) async-start(), calls=%async_computation.3 | async-start | bytes 28311552 | tf_op jit(solution)/shard_map/all_gather | solution.py:37
  93.2 6.9 %copy-start.1 = (bf16[384,6144]{1,0:T(8,128)(2,1)S(1)}, bf16[384,6144]{1,0:T(8,128)(2,1)}, u32[]{:S(2)}) copy-start(bf16[384,6144]{1,0:T(8,128)(2,1)} %all-gather.4.cloned.1.call-done) | copy-start | bytes 14155780
  108.3 1.0 copy-start.2
  108.3 129.3 %copy-start.3 = (bf16[24,6144]{1,0:T(8,128)(2,1)S(1)}, bf16[24,6144]{1,0:T(8,128)(2,1)}, u32[]{:S(2)}) copy-start(bf16[24,6144]{1,0:T(8,128)(2,1)} %param.10) | copy-start | bytes 884740
Sparse Core Ops, SparseCore 0:
  10.8 82.3 all-gather.3
  98.4 137.8 reduce-scatter.1
  238.4 32.5 all-gather.5
